TPU v7x, 32 devices: a whole 2x2x4 slice. The times are simulated.
32 devices in a mesh: angle: 2 (over y), ty: 8 (over z, core), tx: 2 (over x).
Axes of the slice: x: 2, y: 2, z: 4, core: 2. Of those that a mesh axis runs over, the one named last changes fastest.
Arguments:
- object_slices: float32 [2, 2, 2048, 2048], P('angle', None, 'ty', 'tx'), may hold values from -5 to 5
- probe_field: float32 [2, 256, 256], replicated, may hold values from -6 to 6
- positions: int32 [2, 8, 2, 4, 2], P('angle', 'ty', 'tx'), may hold values from 0 to 1792, as said below
- live_slots: int32 [2, 8, 2], P('angle', 'ty', 'tx'), may hold values from 1 to 4, as said below
- photon_counts: int32 [2, 8, 2, 4, 256, 256], P('angle', 'ty', 'tx'), may hold values from 1 to 1600
Outputs:
- new_object: float32 [2, 2, 2048, 2048], P('angle', None, 'ty', 'tx')
- new_probe: float32 [2, 256, 256], P(None, 'ty')
Inputs may be any that keep to these rules, and one draw needn't show every extreme that they name: `positions`: A slot's patch lies inside the object and its centre (top-left plus 128) lies in the rows and columns of the tile that holds the slot: rows r * 256 to (r + 1) * 256 - 1, columns c * 1024 to (c + 1) * 1024 - 1. `live_slots`: some tile of every draw uses all 4 slots.
All inputs are finite; a program needn't handle non-finite values.
Results may differ from a plain program's by a relative error of at most 0.0003.
Values sent between devices are 32-bit elements; how exact they have to be, the bound alone decides.
A program may use at most 128 MiB of HBM per device.

v0:
```python
import functools
import math

import jax
import jax.numpy as jnp
import numpy as np
from jax import lax
from jax.experimental import pallas as pl
from jax.experimental.pallas import tpu as pltpu
from jax.sharding import PartitionSpec as P

MESH = pl.DeviceIdType.MESH
VMEM_LIMIT = 56 * 1024 * 1024
AROUND = tuple((dy, dx) for dy in (-1, 0, 1) for dx in (-1, 0, 1))
BESIDE = tuple(d for d in AROUND if d != (0, 0))


def slot_of(dy, dx):
    return (dy + 1) * 3 + dx + 1


def present(dy, dx, shape):
    row = lax.axis_index("ty") + dy
    col = lax.axis_index("tx") + dx
    return (row >= 0) & (row < shape["ty"]) & (col >= 0) & (col < shape["tx"])


def beside_counts(shape):
    found = []
    for axis in ("ty", "tx"):
        at = lax.axis_index(axis)
        found.append(jnp.where(at > 0, 1, 0) + jnp.where(at < shape[axis] - 1, 1, 0))
    return found


def neighbour(dy, dx):
    return {"ty": lax.axis_index("ty") + dy, "tx": lax.axis_index("tx") + dx}


def edge_part(step, size, half):
    return {-1: slice(0, half), 0: slice(0, size), 1: slice(size - half, size)}[step]


def wide_part(step, size, half):
    return {
        -1: slice(0, half),
        0: slice(half, half + size),
        1: slice(half + size, size + 2 * half),
    }[step]


def at2(ref, rows, cols):
    return ref.at[:, pl.ds(rows.start, rows.stop - rows.start), pl.ds(cols.start, cols.stop - cols.start)]


def halo_kernel(shape, half, tile, meta, wide, metas, send, recv, msend, mrecv, local):
    rows, cols = tile.shape[1], tile.shape[2]
    barrier = pltpu.get_barrier_semaphore()
    for dy, dx in BESIDE:
        @pl.when(present(dy, dx, shape))
        def _():
            pl.semaphore_signal(barrier, inc=1, device_id=neighbour(dy, dx), device_id_type=MESH)
    centre = at2(wide, wide_part(0, rows, half), wide_part(0, cols, half))
    own = pltpu.make_async_copy(tile, centre, local.at[0])
    own.start()
    own_meta = pltpu.make_async_copy(meta, metas.at[4], local.at[1])
    own_meta.start()
    n_row, n_col = beside_counts(shape)
    pl.semaphore_wait(barrier, n_row + n_col + n_row * n_col)

    def copies(dy, dx, k):
        src = at2(tile, edge_part(dy, rows, half), edge_part(dx, cols, half))
        dst = at2(wide, wide_part(-dy, rows, half), wide_part(-dx, cols, half))
        data = pltpu.make_async_remote_copy(
            src_ref=src, dst_ref=dst, send_sem=send.at[k], recv_sem=recv.at[k],
            device_id=neighbour(dy, dx), device_id_type=MESH)
        note = pltpu.make_async_remote_copy(
            src_ref=meta, dst_ref=metas.at[slot_of(-dy, -dx)], send_sem=msend.at[k],
            recv_sem=mrecv.at[k], device_id=neighbour(dy, dx), device_id_type=MESH)
        return data, note

    order = sorted(BESIDE, key=lambda d: abs(d[1]))
    for dy, dx in order:
        @pl.when(present(dy, dx, shape))
        def _():
            data, note = copies(dy, dx, slot_of(dy, dx))
            data.start()
            note.start()
    for dy, dx in order:
        @pl.when(present(dy, dx, shape))
        def _():
            data, note = copies(dy, dx, slot_of(dy, dx))
            data.wait_send()
            note.wait_send()
            data, note = copies(-dy, -dx, slot_of(-dy, -dx))
            data.wait_recv()
            note.wait_recv()
    own.wait()
    own_meta.wait()


def split(value):
    high = value.astype(jnp.bfloat16)
    low = (value - high.astype(jnp.float32)).astype(jnp.bfloat16)
    return high, low


def mm(a, b):
    return lax.dot_general(a, b, (((1,), (0,)), ((), ())), preferred_element_type=jnp.float32)


def compute_kernel(shape, tile_rows, tile_cols, metas, wide_in, probe, counts, tables,
                   tot_out, den, den_max, sums, acc, denbuf, u_hi, u_lo, v_hi, v_lo, wide, tot,
                   load_sem, save_sem):
    size = probe.shape[1]
    half = size // 2
    blocks = wide.shape[1]

    def strip(ref, j):
        return ref.at[:, :, pl.ds(j * 128, 128)]

    def load(j):
        return pltpu.make_async_copy(strip(wide_in, j), wide.at[:, j], load_sem.at[j])

    def save(j):
        return pltpu.make_async_copy(tot.at[:, j], strip(tot_out, j), save_sem.at[j])

    for j in range(blocks):
        load(j).start()
    slots = counts.shape[0]
    ty, tx = lax.axis_index("ty"), lax.axis_index("tx")
    for n, (u, v) in enumerate(((u_hi, v_hi), (u_lo, v_lo))):
        c, s = tables[2 * n], tables[2 * n + 1]
        u[0:size, 0:size] = c
        u[0:size, size:] = s
        u[size:, 0:size] = -s
        u[size:, size:] = c
        v[0:size, 0:size] = c
        v[0:size, size:] = -s
        v[size:, 0:size] = s
        v[size:, size:] = c
    tot[...] = jnp.zeros_like(tot)
    acc[...] = jnp.zeros_like(acc)
    edge = size // 128
    inner = slice(edge, edge + tile_cols // 128)
    denbuf[inner, size:size + tile_rows, :] = jnp.zeros((tile_cols // 128, tile_rows, 128), jnp.float32)
    pad = jnp.zeros((size, 128), jnp.float32)
    wider = size + 128

    def spread(piece, shift):
        return pltpu.roll(jnp.concatenate([piece, pad], axis=1), shift, axis=1)

    def from_left(m_hi, m_lo, re, im):
        hi, lo = split(jnp.concatenate([re, im], axis=0))
        out = mm(m_hi[...], hi) + (mm(m_hi[...], lo) + mm(m_lo[...], hi))
        return out[:size], out[size:]

    def from_right(m_hi, m_lo, re, im):
        hi, lo = split(jnp.concatenate([re, im], axis=1))
        out = mm(hi, m_hi[...]) + (mm(lo, m_hi[...]) + mm(hi, m_lo[...]))
        return out[:, :size], out[:, size:]

    def one_den(n, carry):
        k, s = n // slots, n % slots
        row = metas[k, 0, s] - ty * tile_rows
        col = metas[k, 0, slots + s] - tx * tile_cols
        there_r, there_c = ty + k // 3 - 1, tx + k % 3 - 1
        there = (there_r >= 0) & (there_r < shape["ty"]) & (there_c >= 0) & (there_c < shape["tx"])
        meets = (row > -size) & (row < tile_rows) & (col > -size) & (col < tile_cols)

        @pl.when(there & meets & (s < metas[k, 0, 2 * slots]))
        def _():
            q = probe[0] * probe[0] + probe[1] * probe[1]
            at = col + size
            value = spread(q, at % 128)
            for i in range(wider // 128):
                where = (at // 128 + i, pl.ds(row + size, size), slice(None))
                denbuf[where] += value[:, i * 128:(i + 1) * 128]
        return carry

    lax.fori_loop(0, 9 * slots, one_den, 0)
    own = denbuf[inner, size:size + tile_rows, :]
    for j in range(tile_cols // 128):
        den[:, j * 128:(j + 1) * 128] = own[j]
    most = jnp.max(own, axis=0)
    den_max[...] = jnp.broadcast_to(jnp.max(jnp.max(most, axis=0, keepdims=True), axis=1, keepdims=True), den_max.shape)
    for j in range(blocks):
        load(j).wait()

    def one_slot(s, carry):
        row = metas[4, 0, s] - ty * tile_rows + half
        at = metas[4, 0, slots + s] - tx * tile_cols + half
        first = at // 128
        shift = at % 128
        back_shift = (wider - shift) % wider

        def patch(ch):
            found = [wide[ch, first + i, pl.ds(row, size), :] for i in range(wider // 128)]
            return pltpu.roll(jnp.concatenate(found, axis=1), back_shift, axis=1)[:, :size]

        def deposit(ch, piece):
            value = spread(piece, shift)
            for i in range(wider // 128):
                tot[ch, first + i, pl.ds(row, size), :] += value[:, i * 128:(i + 1) * 128]

        x_re, x_im = patch(0), patch(1)
        q_re, q_im = probe[0], probe[1]
        p_re = q_re * x_re - q_im * x_im
        p_im = q_re * x_im + q_im * x_re
        f_re, f_im = from_right(v_hi, v_lo, *from_left(u_hi, u_lo, p_re, p_im))
        amplitude = 0.05 * jnp.sqrt(counts[s].astype(jnp.float32))
        factor = amplitude * lax.rsqrt(jnp.maximum(f_re * f_re + f_im * f_im, 0.0625))
        b_re, b_im = from_right(u_hi, u_lo, *from_left(v_hi, v_lo, f_re * factor, f_im * factor))
        d_re, d_im = b_re - p_re, b_im - p_im
        deposit(0, q_re * d_re + q_im * d_im)
        deposit(1, q_re * d_im - q_im * d_re)
        acc[0] += x_re * d_re + x_im * d_im
        acc[1] += x_re * d_im - x_im * d_re
        acc[2] += x_re * x_re + x_im * x_im
        return carry

    lax.fori_loop(0, metas[4, 0, 2 * slots], one_slot, 0)
    for j in range(blocks):
        save(j).start()
    each = size // shape["ty"]
    for t in range(shape["ty"]):
        for ch in range(3):
            sums[t % 2, t // 2, ch * each:(ch + 1) * each, :] = acc[ch, t * each:(t + 1) * each, :]
    for j in range(blocks):
        save(j).wait()


def fold_kernel(shape, half, tile, tot, den, den_max, sums, probe_rows, out, out_probe,
                centre, rim_v, rim_h, rim_c, r1, s1, r2, s2, r3, s3, g4, pk_a, pk_b, pk_c,
                fsend, frecv, send1, recv1, send2, recv2, send3, recv3, send4, recv4,
                ksend, krecv, lsend, lrecv, msend, mrecv, local):
    rows, cols = tile.shape[1], tile.shape[2]
    n_ty, n_tx, n_an = shape["ty"], shape["tx"], shape["angle"]
    ty, tx, an = lax.axis_index("ty"), lax.axis_index("tx"), lax.axis_index("angle")
    core, z = ty % 2, ty // 2
    n_z = n_ty // 2
    group = n_an * n_tx
    gid = an * n_tx + tx
    part = sums.shape[3] // n_an
    diagonals = [d for d in BESIDE if d[0] and d[1]]
    barrier = pltpu.get_barrier_semaphore()

    def signal(where):
        pl.semaphore_signal(barrier, inc=1, device_id=where, device_id_type=MESH)

    def member(d):
        g = (gid + d) % group
        return g, {"angle": g // n_tx, "tx": g % n_tx}

    for d in range(1, n_ty):
        signal({"ty": (ty + d) % n_ty})
    for d in range(1, group):
        signal(member(d)[1])
    for dy, dx in diagonals:
        @pl.when(present(dy, dx, shape))
        def _():
            signal(neighbour(dy, dx))
    load = pltpu.make_async_copy(
        at2(tot, wide_part(0, rows, half), wide_part(0, cols, half)), centre, local.at[0])
    load.start()
    n_row, n_col = beside_counts(shape)
    pl.semaphore_wait(barrier, n_ty - 1 + group - 1 + n_row * n_col)

    def rdma(src, dst, s_sem, r_sem, where):
        return pltpu.make_async_remote_copy(
            src_ref=src, dst_ref=dst, send_sem=s_sem, recv_sem=r_sem,
            device_id=where, device_id_type=MESH)

    def landing(dy, dx):
        if dx == 0:
            return rim_v.at[(dy + 1) // 2]
        if dy == 0:
            return rim_h.at[(dx + 1) // 2]
        return rim_c.at[(dy + 1) + (dx + 1) // 2]

    def fold(dy, dx):
        k = slot_of(dy, dx)
        src = at2(tot, wide_part(dy, rows, half), wide_part(dx, cols, half))
        return rdma(src, landing(dy, dx), fsend.at[k], frecv.at[k], neighbour(dy, dx))

    pair = {"ty": ty + 1 - 2 * core}
    c1 = rdma(sums.at[1 - core], r1, send1.at[0], recv1.at[0], pair)
    c1.start()
    for d in range(1, group):
        g, where = member(d)
        rdma(den_max, pk_a.at[gid], ksend.at[d], krecv.at[gid], where).start()
    for dy, dx in sorted(BESIDE, key=lambda d: abs(d[1])):
        @pl.when(present(dy, dx, shape))
        def _():
            fold(dy, dx).start()

    pk_a[pl.ds(gid, 1)] = den_max[...][None]
    c1.wait()
    s1[...] = sums[core] + r1[...]

    def lanes(ref, a):
        return ref.at[:, :, pl.ds(pl.multiple_of(a * part, part), part)]

    def stage2(d):
        a = (an + d) % n_an
        return rdma(lanes(s1, a), r2.at[an], send2.at[d], recv2.at[an], {"angle": a})

    for d in range(1, n_an):
        stage2(d).start()
    for d in range(1, group):
        g, where = member(d)
        rdma(den_max, pk_a.at[g], ksend.at[d], krecv.at[g], where).wait()
    peak = pk_a[0]
    for g in range(1, group):
        peak = jnp.maximum(peak, pk_a[g])
    pk_b[pl.ds(ty, 1)] = peak[None]
    for d in range(1, n_ty):
        rdma(pk_b.at[ty], pk_b.at[ty], lsend.at[d], lrecv.at[ty], {"ty": (ty + d) % n_ty}).start()
    for d in range(1, n_an):
        a = (an + d) % n_an
        rdma(lanes(s1, a), r2.at[a], send2.at[d], recv2.at[a], {"angle": a}).wait()
    mine = s1[:, :, pl.ds(pl.multiple_of(an * part, part), part)]
    for d in range(1, n_an):
        mine = mine + r2[(an + d) % n_an]
    s2[...] = mine

    for d in range(1, n_z):
        o = (z + d) % n_z
        rdma(s2.at[o], r3.at[z], send3.at[d], recv3.at[z], {"ty": o * 2 + core}).start()
    for d in range(1, n_z):
        o = (z + d) % n_z
        rdma(s2.at[o], r3.at[o], send3.at[d], recv3.at[o], {"ty": o * 2 + core}).wait()
    total = s2[z]
    for d in range(1, n_z):
        total = total + r3[(z + d) % n_z]
    s3[...] = total
    g4[pl.ds(gid, 1)] = total[None]

    for d in range(1, group):
        g, where = member(d)
        rdma(s3, g4.at[gid], send4.at[d], recv4.at[gid], where).start()
    for d in range(1, group):
        g, where = member(d)
        rdma(s3, g4.at[g], send4.at[d], recv4.at[g], where).wait()
    pieces = []
    for a in range(n_an):
        piece = g4[a * n_tx]
        for t in range(1, n_tx):
            piece = piece + g4[a * n_tx + t]
        pieces.append(piece)
    full = jnp.concatenate(pieces, axis=1)
    each = full.shape[0] // 3
    p_re, p_im, p_den = full[:each], full[each:2 * each], full[2 * each:]

    def top(value):
        return jnp.max(jnp.max(value, axis=0, keepdims=True), axis=1, keepdims=True)

    pk_c[pl.ds(ty, 1)] = jnp.broadcast_to(top(p_den), den_max.shape)[None]
    for d in range(1, n_ty):
        rdma(pk_c.at[ty], pk_c.at[ty], msend.at[d], mrecv.at[ty], {"ty": (ty + d) % n_ty}).start()

    load.wait()
    for dy, dx in sorted(BESIDE, key=lambda d: -abs(d[1])):
        @pl.when(present(dy, dx, shape))
        def _():
            fold(dy, dx).wait_send()
            fold(-dy, -dx).wait_recv()
            r, c = edge_part(dy, rows, half), edge_part(dx, cols, half)
            centre[:, r, c] += landing(-dy, -dx)[...]
    for d in range(1, n_ty):
        o = (ty + d) % n_ty
        rdma(pk_b.at[ty], pk_b.at[o], lsend.at[d], lrecv.at[o], {"ty": o}).wait()
    peak = pk_b[0]
    for t in range(1, n_ty):
        peak = jnp.maximum(peak, pk_b[t])
    scale = 1.0 / (den[...] + 0.1 * peak[0:1, 0:1])
    out[0] = tile[0] + centre[0] * scale
    out[1] = tile[1] + centre[1] * scale

    for d in range(1, n_ty):
        o = (ty + d) % n_ty
        rdma(pk_c.at[ty], pk_c.at[o], msend.at[d], mrecv.at[o], {"ty": o}).wait()
    peak = pk_c[0]
    for t in range(1, n_ty):
        peak = jnp.maximum(peak, pk_c[t])
    scale = 1.0 / (p_den + 0.1 * peak[0:1, 0:1])
    out_probe[0] = probe_rows[0] + p_re * scale
    out_probe[1] = probe_rows[1] + p_im * scale


def table_values(length):
    ids = np.arange(length)
    phase = 2.0 * math.pi / length * (np.outer(ids, ids) % length)
    cos, sin = np.cos(phase) / math.sqrt(length), np.sin(phase) / math.sqrt(length)
    parts = []
    for value in (cos, sin):
        high = value.astype(jnp.bfloat16)
        low = (value - high.astype(np.float64)).astype(jnp.bfloat16)
        parts.append((high, low))
    return np.stack([parts[0][0], parts[1][0], parts[0][1], parts[1][1]])


def body(shape, object_slices, probe_field, positions, live_slots, photon_counts):
    f32 = jnp.float32
    dma = pltpu.SemaphoreType.DMA
    size = probe_field.shape[1]
    half = size // 2
    tile = object_slices[0]
    _, rows, cols = tile.shape
    spots = positions[0, 0, 0]
    slots = spots.shape[0]
    vmem = pl.BlockSpec(memory_space=pltpu.VMEM)
    smem = pl.BlockSpec(memory_space=pltpu.SMEM)
    anywhere = pl.BlockSpec(memory_space=pl.ANY)
    line = jnp.concatenate([spots[:, 0], spots[:, 1], live_slots[0, 0]])
    meta = jnp.broadcast_to(jnp.pad(line, (0, 128 - line.shape[0]))[None], (8, 128))
    wide, metas = pl.pallas_call(
        functools.partial(halo_kernel, shape, half),
        out_shape=(
            jax.ShapeDtypeStruct((2, rows + size, cols + size), f32),
            jax.ShapeDtypeStruct((9, 8, 128), jnp.int32),
        ),
        in_specs=[vmem, vmem],
        out_specs=(anywhere, anywhere),
        scratch_shapes=[dma((9,)), dma((9,)), dma((9,)), dma((9,)), dma((2,))],
        compiler_params=pltpu.CompilerParams(
            collective_id=0, has_side_effects=True, vmem_limit_bytes=VMEM_LIMIT),
    )(tile, meta)

    n_ty, n_tx, n_an = shape["ty"], shape["tx"], shape["angle"]
    n_z, each, group = n_ty // 2, size // n_ty, n_an * n_tx
    part = size // n_an
    tot, den, den_max, sums = pl.pallas_call(
        functools.partial(compute_kernel, shape, rows, cols),
        out_shape=(
            jax.ShapeDtypeStruct((2, rows + size, cols + size), f32),
            jax.ShapeDtypeStruct((rows, cols), f32),
            jax.ShapeDtypeStruct((8, 128), f32),
            jax.ShapeDtypeStruct((2, n_z, 3 * each, size), f32),
        ),
        in_specs=[smem, anywhere, vmem, vmem, vmem],
        out_specs=(anywhere, vmem, vmem, vmem),
        scratch_shapes=[
            pltpu.VMEM((3, size, size), f32),
            pltpu.VMEM(((cols + 2 * size) // 128, rows + 2 * size, 128), f32),
        ] + [pltpu.VMEM((2 * size, 2 * size), jnp.bfloat16)] * 4 + [
            pltpu.VMEM((2, (cols + size) // 128, rows + size, 128), f32)] * 2 + [
            dma(((cols + size) // 128,))] * 2,
        compiler_params=pltpu.CompilerParams(vmem_limit_bytes=VMEM_LIMIT),
    )(metas, wide, probe_field, photon_counts[0, 0, 0], jnp.asarray(table_values(size)))

    probe_rows = lax.dynamic_slice_in_dim(probe_field, lax.axis_index("ty") * each, each, 1)
    return pl.pallas_call(
        functools.partial(fold_kernel, shape, half),
        out_shape=(
            jax.ShapeDtypeStruct((2, rows, cols), f32),
            jax.ShapeDtypeStruct((2, each, size), f32),
        ),
        in_specs=[vmem, anywhere, vmem, vmem, vmem, vmem],
        out_specs=(vmem, vmem),
        scratch_shapes=[
            pltpu.VMEM((2, rows, cols), f32),
            pltpu.VMEM((2, 2, half, cols), f32),
            pltpu.VMEM((2, 2, rows, half), f32),
            pltpu.VMEM((4, 2, half, half), f32),
            pltpu.VMEM((n_z, 3 * each, size), f32),
            pltpu.VMEM((n_z, 3 * each, size), f32),
            pltpu.VMEM((n_an, n_z, 3 * each, part), f32),
            pltpu.VMEM((n_z, 3 * each, part), f32),
            pltpu.VMEM((n_z, 3 * each, part), f32),
            pltpu.VMEM((3 * each, part), f32),
            pltpu.VMEM((group, 3 * each, part), f32),
            pltpu.VMEM((group, 8, 128), f32),
            pltpu.VMEM((n_ty, 8, 128), f32),
            pltpu.VMEM((n_ty, 8, 128), f32),
            dma((9,)), dma((9,)), dma((1,)), dma((1,)), dma((n_an,)), dma((n_an,)),
            dma((n_z,)), dma((n_z,)), dma((group,)), dma((group,)),
            dma((group,)), dma((group,)), dma((n_ty,)), dma((n_ty,)), dma((n_ty,)), dma((n_ty,)),
            dma((1,)),
        ],
        compiler_params=pltpu.CompilerParams(
            collective_id=1, has_side_effects=True, vmem_limit_bytes=VMEM_LIMIT),
    )(tile, tot, den, den_max, sums, probe_rows)


def solution(mesh):
    shape = dict(mesh.shape)

    def step(*args):
        new_tile, new_probe = body(shape, *args)
        return new_tile[None], new_probe

    return jax.shard_map(
        step,
        mesh=mesh,
        in_specs=(
            P("angle", None, "ty", "tx"),
            P(),
            P("angle", "ty", "tx", None, None),
            P("angle", "ty", "tx"),
            P("angle", "ty", "tx", None, None, None),
        ),
        out_specs=(P("angle", None, "ty", "tx"), P(None, "ty", None)),
        check_vma=False,
    )
```

profile of v0, /device:TPU:0, one launch (start us, length us, event | category | flops | bytes accessed | tf_op | source)
XLA Modules:
  0.0 88.1 jit_solution(9478049016246481577)
XLA Ops:
  0.6 0.8 slice_bitcast_fusion.1
  2.0 0.1 pad_add_fusion
  2.1 0.6 broadcast_in_dim.4.meta
  2.7 14.1 %shard_map.77 = (f32[2,512,1280]{2,1,0:T(8,128)}, s32[9,8,128]{2,1,0:T(8,128)}) custom-call(f32[2,256,1024]{2,1,0:T(8,128)} %bitcast.10, s32[8,128]{1,0:T(8,128)} %broadcast_in_dim.4.meta), custom_call_target="tpu_custom_call" | custom-call | tf_op jit(solution)/shard_map/pallas_call | solution.py:417
  16.9 11.9 %shard_map.78 = (f32[2,512,1280]{2,1,0:T(8,128)}, f32[256,1024]{1,0:T(8,128)}, f32[8,128]{1,0:T(8,128)}, f32[2,4,96,256]{3,2,1,0:T(8,128)}) custom-call(s32[9,8,128]{2,1,0:T(8,128)} %get-tuple-element.10.metas, f32[2,512,1280]{2,1,0:T(8,128)} %get-tuple-element.11.wide_in, f32[2,256,256]{2,1,0:T(8,128)} %probe.1, s32[4,256,256]{2,1,0:T(8,128)} %bitcast.13, ...), custom_call_target="tpu_custom_call" | custom-call | tf_op jit(solution)/shard_map/pallas_call | solution.py:433
  28.8 1.5 %constant_dynamic-slice_fusion.probe_rows = f32[2,32,256]{2,1,0:T(8,128)} fusion(f32[2,256,256]{2,1,0:T(8,128)} %probe.1, s32[]{:T(128)S(6)} %select_n.3), kind=kLoop, calls=%fused_computation.3 | loop fusion | bytes 131076 | tf_op jit(solution)/shard_map/dynamic_slice | solution.py:452
  30.2 54.0 %shard_map.79 = (f32[2,256,1024]{2,1,0:T(8,128)}, f32[2,32,256]{2,1,0:T(8,128)}) custom-call(f32[2,256,1024]{2,1,0:T(8,128)} %bitcast.11, f32[2,512,1280]{2,1,0:T(8,128)} %get-tuple-element.12.tot, f32[256,1024]{1,0:T(8,128)} %get-tuple-element.13.den, f32[8,128]{1,0:T(8,128)} %get-tuple-element.14.den_max, f32[2,4,96,256]{3,2,1,0:T(8,128)} %get-tuple-element.15.sums, ...), custom_call_target="tpu_custom_call" | custom-call | tf_op jit(solution)/shard_map/pallas_call | solution.py:453
  84.3 0.0 copy-start
  84.3 3.2 %copy.11 = f32[1,2,256,1024]{3,2,1,0:T(8,128)} copy(f32[1,2,256,1024]{3,2,1,0:T(8,128)} %bitcast.12) | data formatting | bytes 4194304
  87.5 0.0 copy-done
  87.5 0.6 copy.12
  (1 shorter events, 0.0 us)
Async XLA Ops:
  84.3 3.2 %copy-start = (f32[2,32,256]{2,1,0:T(8,128)S(1)}, f32[2,32,256]{2,1,0:T(8,128)}, u32[]{:S(2)}) copy-start(f32[2,32,256]{2,1,0:T(8,128)} %get-tuple-element.23) | copy-start | bytes 196612
where the time goes:
time: 88.3 us; the launch traced here: 88.1 us
  Pallas kernels  80 us (91%)
  local copies, waits for them, and re-layouts  6.67 us (8%)
  between operations  1.32 us (1%)
    pallas_call x1, Pallas kernels, body(): pl.pallas_call(functools.partial(fold_kernel, shape, half), out_shape=(ja...  54 us
    pallas_call x1, Pallas kernels, body(): pl.pallas_call(functools.partial(halo_kernel, shape, half), out_shape=(ja...  14.1 us
    pallas_call x1, Pallas kernels, body(): pl.pallas_call(functools.partial(compute_kernel, shape, rows, cols), out_...  11.9 us
    unnamed x4, local copies, waits for them, and re-layouts  3.82 us

commit v1 on v0

--- a/solution.py
+++ b/solution.py
@@ -10,7 +10,10 @@
 from jax.sharding import PartitionSpec as P
 
 MESH = pl.DeviceIdType.MESH
-VMEM_LIMIT = 56 * 1024 * 1024
+MIB = 1024 * 1024
+HALO_VMEM = 4 * MIB
+VMEM_LIMIT = 32 * MIB
+FOLD_VMEM = 14 * MIB
 AROUND = tuple((dy, dx) for dy in (-1, 0, 1) for dx in (-1, 0, 1))
 BESIDE = tuple(d for d in AROUND if d != (0, 0))
 
@@ -60,9 +63,6 @@
         @pl.when(present(dy, dx, shape))
         def _():
             pl.semaphore_signal(barrier, inc=1, device_id=neighbour(dy, dx), device_id_type=MESH)
-    centre = at2(wide, wide_part(0, rows, half), wide_part(0, cols, half))
-    own = pltpu.make_async_copy(tile, centre, local.at[0])
-    own.start()
     own_meta = pltpu.make_async_copy(meta, metas.at[4], local.at[1])
     own_meta.start()
     n_row, n_col = beside_counts(shape)
@@ -95,7 +95,6 @@
             data, note = copies(-dy, -dx, slot_of(-dy, -dx))
             data.wait_recv()
             note.wait_recv()
-    own.wait()
     own_meta.wait()
 
 
@@ -109,7 +108,7 @@
     return lax.dot_general(a, b, (((1,), (0,)), ((), ())), preferred_element_type=jnp.float32)
 
 
-def compute_kernel(shape, tile_rows, tile_cols, metas, wide_in, probe, counts, tables,
+def compute_kernel(shape, tile_rows, tile_cols, metas, tile_in, wide_in, probe, counts, tables,
                    tot_out, den, den_max, sums, acc, denbuf, u_hi, u_lo, v_hi, v_lo, wide, tot,
                    load_sem, save_sem):
     size = probe.shape[1]
@@ -119,14 +118,31 @@
     def strip(ref, j):
         return ref.at[:, :, pl.ds(j * 128, 128)]
 
-    def load(j):
-        return pltpu.make_async_copy(strip(wide_in, j), wide.at[:, j], load_sem.at[j])
+    inside = range(half // 128, blocks - half // 128)
+
+    def band(ref, j, start, count):
+        return ref.at[:, pl.ds(start, count), pl.ds(j * 128, 128)]
+
+    def loads(j):
+        if j not in inside:
+            return [pltpu.make_async_copy(strip(wide_in, j), wide.at[:, j], load_sem.at[j, 0])]
+        low = half + tile_rows
+        return [
+            pltpu.make_async_copy(
+                band(tile_in, j - inside[0], 0, tile_rows),
+                wide.at[:, j, pl.ds(half, tile_rows), :], load_sem.at[j, 0]),
+            pltpu.make_async_copy(
+                band(wide_in, j, 0, half), wide.at[:, j, pl.ds(0, half), :], load_sem.at[j, 1]),
+            pltpu.make_async_copy(
+                band(wide_in, j, low, half), wide.at[:, j, pl.ds(low, half), :], load_sem.at[j, 2]),
+        ]
 
     def save(j):
         return pltpu.make_async_copy(tot.at[:, j], strip(tot_out, j), save_sem.at[j])
 
     for j in range(blocks):
-        load(j).start()
+        for copy in loads(j):
+            copy.start()
     slots = counts.shape[0]
     ty, tx = lax.axis_index("ty"), lax.axis_index("tx")
     for n, (u, v) in enumerate(((u_hi, v_hi), (u_lo, v_lo))):
@@ -185,7 +201,8 @@
     most = jnp.max(own, axis=0)
     den_max[...] = jnp.broadcast_to(jnp.max(jnp.max(most, axis=0, keepdims=True), axis=1, keepdims=True), den_max.shape)
     for j in range(blocks):
-        load(j).wait()
+        for copy in loads(j):
+            copy.wait()
 
     def one_slot(s, carry):
         row = metas[4, 0, s] - ty * tile_rows + half
@@ -230,8 +247,8 @@
         save(j).wait()
 
 
-def fold_kernel(shape, half, tile, tot, den, den_max, sums, probe_rows, out, out_probe,
-                centre, rim_v, rim_h, rim_c, r1, s1, r2, s2, r3, s3, g4, pk_a, pk_b, pk_c,
+def fold_kernel(shape, half, tile_in, tot, den_in, den_max, sums, probe_in, out, out_probe,
+                tile, den, probe_rows, s0, centre, rim_v, rim_h, rim_c, r1, s1, r2, s2, r3, s3, g4, pk_a, pk_b, pk_c,
                 fsend, frecv, send1, recv1, send2, recv2, send3, recv3, send4, recv4,
                 ksend, krecv, lsend, lrecv, msend, mrecv, local):
     rows, cols = tile.shape[1], tile.shape[2]
@@ -260,9 +277,16 @@
         @pl.when(present(dy, dx, shape))
         def _():
             signal(neighbour(dy, dx))
+    each = probe_rows.shape[1]
+    own_rows = pl.ds(pl.multiple_of(ty * each, each), each)
     load = pltpu.make_async_copy(
         at2(tot, wide_part(0, rows, half), wide_part(0, cols, half)), centre, local.at[0])
-    load.start()
+    load_sums = pltpu.make_async_copy(sums.at[core], s0, local.at[1])
+    load_tile = pltpu.make_async_copy(tile_in, tile, local.at[2])
+    load_den = pltpu.make_async_copy(den_in, den, local.at[3])
+    load_probe = pltpu.make_async_copy(probe_in.at[:, own_rows, :], probe_rows, local.at[4])
+    for copy in (load_sums, load, load_tile, load_den, load_probe):
+        copy.start()
     n_row, n_col = beside_counts(shape)
     pl.semaphore_wait(barrier, n_ty - 1 + group - 1 + n_row * n_col)
 
@@ -278,10 +302,23 @@
             return rim_h.at[(dx + 1) // 2]
         return rim_c.at[(dy + 1) + (dx + 1) // 2]
 
-    def fold(dy, dx):
-        k = slot_of(dy, dx)
-        src = at2(tot, wide_part(dy, rows, half), wide_part(dx, cols, half))
-        return rdma(src, landing(dy, dx), fsend.at[k], frecv.at[k], neighbour(dy, dx))
+    early = half * 5 // 8 // 8 * 8
+
+    def fold(dy, dx, piece=0):
+        k = slot_of(dy, dx) + 9 * piece
+        part_rows, part_cols = wide_part(dy, rows, half), wide_part(dx, cols, half)
+        place = landing(dy, dx)
+        if dx == 0:
+            begin, stop = (0, early) if piece == 0 else (early, half)
+            part_rows = slice(part_rows.start + begin, part_rows.start + stop)
+            place = place.at[:, pl.ds(begin, stop - begin), :]
+        return rdma(at2(tot, part_rows, part_cols), place, fsend.at[k], frecv.at[k], neighbour(dy, dx))
+
+    def start_folds(which):
+        for dy, dx, piece in which:
+            @pl.when(present(dy, dx, shape))
+            def _():
+                fold(dy, dx, piece).start()
 
     pair = {"ty": ty + 1 - 2 * core}
     c1 = rdma(sums.at[1 - core], r1, send1.at[0], recv1.at[0], pair)
@@ -289,14 +326,12 @@
     for d in range(1, group):
         g, where = member(d)
         rdma(den_max, pk_a.at[gid], ksend.at[d], krecv.at[gid], where).start()
-    for dy, dx in sorted(BESIDE, key=lambda d: abs(d[1])):
-        @pl.when(present(dy, dx, shape))
-        def _():
-            fold(dy, dx).start()
+    start_folds([(-1, 0, 0), (1, 0, 0), (0, -1, 0), (0, 1, 0)])
 
     pk_a[pl.ds(gid, 1)] = den_max[...][None]
     c1.wait()
-    s1[...] = sums[core] + r1[...]
+    load_sums.wait()
+    s1[...] = s0[...] + r1[...]
 
     def lanes(ref, a):
         return ref.at[:, :, pl.ds(pl.multiple_of(a * part, part), part)]
@@ -327,6 +362,7 @@
     for d in range(1, n_z):
         o = (z + d) % n_z
         rdma(s2.at[o], r3.at[z], send3.at[d], recv3.at[z], {"ty": o * 2 + core}).start()
+    start_folds([(-1, 0, 1), (1, 0, 1)] + [(dy, dx, 0) for dy, dx in diagonals])
     for d in range(1, n_z):
         o = (z + d) % n_z
         rdma(s2.at[o], r3.at[o], send3.at[d], recv3.at[o], {"ty": o * 2 + core}).wait()
@@ -349,7 +385,6 @@
             piece = piece + g4[a * n_tx + t]
         pieces.append(piece)
     full = jnp.concatenate(pieces, axis=1)
-    each = full.shape[0] // 3
     p_re, p_im, p_den = full[:each], full[each:2 * each], full[2 * each:]
 
     def top(value):
@@ -359,12 +394,14 @@
     for d in range(1, n_ty):
         rdma(pk_c.at[ty], pk_c.at[ty], msend.at[d], mrecv.at[ty], {"ty": (ty + d) % n_ty}).start()
 
-    load.wait()
-    for dy, dx in sorted(BESIDE, key=lambda d: -abs(d[1])):
+    for copy in (load, load_tile, load_den, load_probe):
+        copy.wait()
+    for dy, dx in [(0, -1), (0, 1), (-1, 0), (1, 0)] + diagonals:
         @pl.when(present(dy, dx, shape))
         def _():
-            fold(dy, dx).wait_send()
-            fold(-dy, -dx).wait_recv()
+            for piece in (0, 1) if dx == 0 else (0,):
+                fold(dy, dx, piece).wait_send()
+                fold(-dy, -dx, piece).wait_recv()
             r, c = edge_part(dy, rows, half), edge_part(dx, cols, half)
             centre[:, r, c] += landing(-dy, -dx)[...]
     for d in range(1, n_ty):
@@ -374,8 +411,10 @@
     for t in range(1, n_ty):
         peak = jnp.maximum(peak, pk_b[t])
     scale = 1.0 / (den[...] + 0.1 * peak[0:1, 0:1])
-    out[0] = tile[0] + centre[0] * scale
-    out[1] = tile[1] + centre[1] * scale
+    centre[0] = tile[0] + centre[0] * scale
+    centre[1] = tile[1] + centre[1] * scale
+    store = pltpu.make_async_copy(centre, out, local.at[5])
+    store.start()
 
     for d in range(1, n_ty):
         o = (ty + d) % n_ty
@@ -386,6 +425,7 @@
     scale = 1.0 / (p_den + 0.1 * peak[0:1, 0:1])
     out_probe[0] = probe_rows[0] + p_re * scale
     out_probe[1] = probe_rows[1] + p_im * scale
+    store.wait()
 
 
 def table_values(length):
@@ -420,11 +460,12 @@
             jax.ShapeDtypeStruct((2, rows + size, cols + size), f32),
             jax.ShapeDtypeStruct((9, 8, 128), jnp.int32),
         ),
-        in_specs=[vmem, vmem],
+        in_specs=[anywhere, vmem],
         out_specs=(anywhere, anywhere),
         scratch_shapes=[dma((9,)), dma((9,)), dma((9,)), dma((9,)), dma((2,))],
+        cost_estimate=pl.CostEstimate(flops=10**10, bytes_accessed=4 * tile.size, transcendentals=0),
         compiler_params=pltpu.CompilerParams(
-            collective_id=0, has_side_effects=True, vmem_limit_bytes=VMEM_LIMIT),
+            collective_id=0, has_side_effects=True, vmem_limit_bytes=HALO_VMEM),
     )(tile, meta)
 
     n_ty, n_tx, n_an = shape["ty"], shape["tx"], shape["angle"]
@@ -438,27 +479,30 @@
             jax.ShapeDtypeStruct((8, 128), f32),
             jax.ShapeDtypeStruct((2, n_z, 3 * each, size), f32),
         ),
-        in_specs=[smem, anywhere, vmem, vmem, vmem],
+        in_specs=[smem, anywhere, anywhere, vmem, vmem, vmem],
         out_specs=(anywhere, vmem, vmem, vmem),
         scratch_shapes=[
             pltpu.VMEM((3, size, size), f32),
             pltpu.VMEM(((cols + 2 * size) // 128, rows + 2 * size, 128), f32),
         ] + [pltpu.VMEM((2 * size, 2 * size), jnp.bfloat16)] * 4 + [
             pltpu.VMEM((2, (cols + size) // 128, rows + size, 128), f32)] * 2 + [
-            dma(((cols + size) // 128,))] * 2,
+            dma(((cols + size) // 128, 3)), dma(((cols + size) // 128,))],
         compiler_params=pltpu.CompilerParams(vmem_limit_bytes=VMEM_LIMIT),
-    )(metas, wide, probe_field, photon_counts[0, 0, 0], jnp.asarray(table_values(size)))
-
-    probe_rows = lax.dynamic_slice_in_dim(probe_field, lax.axis_index("ty") * each, each, 1)
+    )(metas, tile, wide, probe_field, photon_counts[0, 0, 0], jnp.asarray(table_values(size)))
+
     return pl.pallas_call(
         functools.partial(fold_kernel, shape, half),
         out_shape=(
             jax.ShapeDtypeStruct((2, rows, cols), f32),
             jax.ShapeDtypeStruct((2, each, size), f32),
         ),
-        in_specs=[vmem, anywhere, vmem, vmem, vmem, vmem],
-        out_specs=(vmem, vmem),
+        in_specs=[anywhere, anywhere, anywhere, vmem, anywhere, anywhere],
+        out_specs=(anywhere, vmem),
         scratch_shapes=[
+            pltpu.VMEM((2, rows, cols), f32),
+            pltpu.VMEM((rows, cols), f32),
+            pltpu.VMEM((2, each, size), f32),
+            pltpu.VMEM((n_z, 3 * each, size), f32),
             pltpu.VMEM((2, rows, cols), f32),
             pltpu.VMEM((2, 2, half, cols), f32),
             pltpu.VMEM((2, 2, rows, half), f32),
@@ -473,14 +517,14 @@
             pltpu.VMEM((group, 8, 128), f32),
             pltpu.VMEM((n_ty, 8, 128), f32),
             pltpu.VMEM((n_ty, 8, 128), f32),
-            dma((9,)), dma((9,)), dma((1,)), dma((1,)), dma((n_an,)), dma((n_an,)),
+            dma((18,)), dma((18,)), dma((1,)), dma((1,)), dma((n_an,)), dma((n_an,)),
             dma((n_z,)), dma((n_z,)), dma((group,)), dma((group,)),
             dma((group,)), dma((group,)), dma((n_ty,)), dma((n_ty,)), dma((n_ty,)), dma((n_ty,)),
-            dma((1,)),
+            dma((6,)),
         ],
         compiler_params=pltpu.CompilerParams(
-            collective_id=1, has_side_effects=True, vmem_limit_bytes=VMEM_LIMIT),
-    )(tile, tot, den, den_max, sums, probe_rows)
+            collective_id=1, has_side_effects=True, vmem_limit_bytes=FOLD_VMEM),
+    )(tile, tot, den, den_max, sums, probe_field)
 
 
 def solution(mesh):

time: 88.3 us -> 74.6 us (0.84)
  Pallas kernels: 80 us -> 68.4 us
  local copies, waits for them, and re-layouts: 6.67 us -> 4.33 us
    pallas_call x1, Pallas kernels: 54 us -> 33.5 us  [body(): pl.pallas_call(functools.partial(fold_kernel, shape, half), out_shape=(ja...]
    pallas_call x1, Pallas kernels: 11.9 us -> 22.3 us  [body(): pl.pallas_call(functools.partial(compute_kernel, shape, rows, cols), out_...]
    pallas_call x1, Pallas kernels: 14.1 us -> 12.6 us  [body(): pl.pallas_call(functools.partial(halo_kernel, shape, half), out_shape=(ja...]
    dynamic_slice x1 -> x0, local copies, waits for them, and re-layouts: 1.48 us -> none  [body(): lax.dynamic_slice_in_dim(probe_field, lax.axis_index('ty') * each, each, 1)]
    unnamed x4 -> x12, local copies, waits for them, and re-layouts: 3.82 us -> 3.56 us
where the time goes in v1:
time: 74.6 us; the launch traced here: 74.2 us
  Pallas kernels  68.4 us (92%)
  local copies, waits for them, and re-layouts  4.33 us (6%)
  between operations  1.34 us (2%)
    pallas_call x1, Pallas kernels, body(): pl.pallas_call(functools.partial(fold_kernel, shape, half), out_shape=(ja...  33.5 us
    pallas_call x1, Pallas kernels, body(): pl.pallas_call(functools.partial(compute_kernel, shape, rows, cols), out_...  22.3 us
    pallas_call x1, Pallas kernels, body(): pl.pallas_call(functools.partial(halo_kernel, shape, half), out_shape=(ja...  12.6 us
    unnamed x12, local copies, waits for them, and re-layouts  3.56 us

profile of v1, /device:TPU:0, one launch (start us, length us, event | category | flops | bytes accessed | tf_op | source)
XLA Modules:
  0.0 74.2 jit_solution(12495593775056570800)
XLA Ops:
  1.3 0.8 %slice_bitcast_fusion.1 = (s32[4]{0:T(128)S(1)}, s32[4]{0:T(128)S(1)}) fusion(s32[4,2]{0,1:T(2,128)} %bitcast.15), kind=kLoop, calls=%fused_computation.2 | loop fusion | bytes 64 | tf_op jit(solution)/shard_map/squeeze | solution.py:455
  2.0 0.1 pad_add_fusion
  2.1 0.0 copy-start
  2.1 1.6 %copy-done = f32[1,2,256,1024]{3,2,1,0:T(8,128)S(1)} copy-done((f32[1,2,256,1024]{3,2,1,0:T(8,128)S(1)}, f32[1,2,256,1024]{3,2,1,0:T(8,128)}, u32[]{:S(2)}) %copy-start) | copy-done | bytes 2097176
  3.7 0.0 copy-start.1
  3.7 0.0 copy-start.2
  3.7 0.0 copy-start.3
  3.7 0.0 copy-start.4
  3.7 12.6 %shard_map.77 = (f32[2,512,1280]{2,1,0:T(8,128)S(1)}, s32[9,8,128]{2,1,0:T(8,128)S(1)}) custom-call(f32[2,256,1024]{2,1,0:T(8,128)S(1)} %bitcast.10, s32[8,128]{1,0:T(8,128)S(1)} %broadcast_in_dim.4.meta), custom_call_target="tpu_custom_call" | custom-call | flops 10000000000 | bytes 2097152 | tf_op jit(solution)/shard_map/pallas_call | solution.py:457
  16.4 0.0 copy-done.1
  16.4 0.0 copy-done.2
  16.4 0.0 copy-done.3
  16.4 0.0 copy-done.4
  16.4 22.3 %shard_map.78 = (f32[2,512,1280]{2,1,0:T(8,128)S(1)}, f32[256,1024]{1,0:T(8,128)S(1)}, f32[8,128]{1,0:T(8,128)S(1)}, f32[2,4,96,256]{3,2,1,0:T(8,128)S(1)}) custom-call(s32[9,8,128]{2,1,0:T(8,128)S(1)} %get-tuple-element.10.metas, f32[2,256,1024]{2,1,0:T(8,128)S(1)} %bitcast.11, f32[2,512,1280]{2,1,0:T(8,128)S(1)} %get-tuple-element.11.wide_in, ...), custom_call_target="tpu_custom_call" | custom-call | tf_op jit(solution)/shard_map/pallas_call | solution.py:474
  38.7 33.5 %shard_map.79 = (f32[2,256,1024]{2,1,0:T(8,128)S(1)}, f32[2,32,256]{2,1,0:T(8,128)S(1)}) custom-call(f32[2,256,1024]{2,1,0:T(8,128)S(1)} %bitcast.12, f32[2,512,1280]{2,1,0:T(8,128)S(1)} %get-tuple-element.12.tot, f32[256,1024]{1,0:T(8,128)S(1)} %get-tuple-element.13.den_in, f32[8,128]{1,0:T(8,128)S(1)} %get-tuple-element.14.den_max, ...), custom_call_target="tpu_custom_call" | custom-call | tf_op jit(solution)/shard_map/pallas_call | solution.py:493
  72.2 1.3 %copy.11 = f32[1,2,256,1024]{3,2,1,0:T(8,128)} copy(f32[1,2,256,1024]{3,2,1,0:T(8,128)S(1)} %bitcast.13) | data formatting | bytes 4194304
  73.5 0.6 copy.12
  (2 shorter events, 0.0 us)
Async XLA Ops:
  2.1 1.6 %copy-start = (f32[1,2,256,1024]{3,2,1,0:T(8,128)S(1)}, f32[1,2,256,1024]{3,2,1,0:T(8,128)}, u32[]{:S(2)}) copy-start(f32[1,2,256,1024]{3,2,1,0:T(8,128)} %param.6) | copy-start | bytes 6291460
  3.7 12.7 %copy-start.1 = (f32[1,2,256,1024]{3,2,1,0:T(8,128)S(1)}, f32[1,2,256,1024]{3,2,1,0:T(8,128)}, u32[]{:S(2)}) copy-start(f32[1,2,256,1024]{3,2,1,0:T(8,128)} %param.6) | copy-start | bytes 6291460
  3.7 12.7 %copy-start.2 = (f32[2,256,256]{2,1,0:T(8,128)S(1)}, f32[2,256,256]{2,1,0:T(8,128)}, u32[]{:S(2)}) copy-start(f32[2,256,256]{2,1,0:T(8,128)} %probe_in.1) | copy-start | bytes 1572868
  3.7 12.7 %copy-start.3 = (s32[1,1,1,4,256,256]{5,4,3,2,1,0:T(8,128)S(1)}, s32[1,1,1,4,256,256]{5,4,3,2,1,0:T(8,128)}, u32[]{:S(2)}) copy-start(s32[1,1,1,4,256,256]{5,4,3,2,1,0:T(8,128)} %param.10) | copy-start | bytes 3145732
  3.7 12.7 %copy-start.4 = (bf16[4,256,256]{2,1,0:T(8,128)(2,1)S(1)}, bf16[4,256,256]{2,1,0:T(8,128)(2,1)}, u32[]{:S(2)}) copy-start(bf16[4,256,256]{2,1,0:T(8,128)(2,1)} %constant.4.clone.tables) | copy-start | bytes 1572868

commit v2 on v1

--- a/solution.py
+++ b/solution.py
@@ -109,7 +109,7 @@
 
 
 def compute_kernel(shape, tile_rows, tile_cols, metas, tile_in, wide_in, probe, counts, tables,
-                   tot_out, den, den_max, sums, acc, denbuf, u_hi, u_lo, v_hi, v_lo, wide, tot,
+                   tot_out, den, den_max, sums, acc, denbuf, u_beside, v_beside, u_below, v_below, wide, tot,
                    load_sem, save_sem):
     size = probe.shape[1]
     half = size // 2
@@ -145,16 +145,14 @@
             copy.start()
     slots = counts.shape[0]
     ty, tx = lax.axis_index("ty"), lax.axis_index("tx")
-    for n, (u, v) in enumerate(((u_hi, v_hi), (u_lo, v_lo))):
-        c, s = tables[2 * n], tables[2 * n + 1]
-        u[0:size, 0:size] = c
-        u[0:size, size:] = s
-        u[size:, 0:size] = -s
-        u[size:, size:] = c
-        v[0:size, 0:size] = c
-        v[0:size, size:] = -s
-        v[size:, 0:size] = s
-        v[size:, size:] = c
+    for n, level in enumerate((0, 0, 1)):
+        c, s = tables[2 * level], tables[2 * level + 1]
+        at = 2 * size * n
+        for beside, below, top_right, low_left in ((u_beside, u_below, s, -s), (v_beside, v_below, -s, s)):
+            quads = ((0, 0, c), (0, size, top_right), (size, 0, low_left), (size, size, c))
+            for row, col, value in quads:
+                beside[row:row + size, at + col:at + col + size] = value
+                below[at + row:at + row + size, col:col + size] = value
     tot[...] = jnp.zeros_like(tot)
     acc[...] = jnp.zeros_like(acc)
     edge = size // 128
@@ -166,14 +164,14 @@
     def spread(piece, shift):
         return pltpu.roll(jnp.concatenate([piece, pad], axis=1), shift, axis=1)
 
-    def from_left(m_hi, m_lo, re, im):
-        hi, lo = split(jnp.concatenate([re, im], axis=0))
-        out = mm(m_hi[...], hi) + (mm(m_hi[...], lo) + mm(m_lo[...], hi))
+    def from_left(m, re, im):
+        (rh, rl), (ih, il) = split(re), split(im)
+        out = mm(m[...], jnp.concatenate([rh, ih, rl, il, rh, ih], axis=0))
         return out[:size], out[size:]
 
-    def from_right(m_hi, m_lo, re, im):
-        hi, lo = split(jnp.concatenate([re, im], axis=1))
-        out = mm(hi, m_hi[...]) + (mm(lo, m_hi[...]) + mm(hi, m_lo[...]))
+    def from_right(m, re, im):
+        (rh, rl), (ih, il) = split(re), split(im)
+        out = mm(jnp.concatenate([rh, ih, rl, il, rh, ih], axis=1), m[...])
         return out[:, :size], out[:, size:]
 
     def one_den(n, carry):
@@ -224,10 +222,10 @@
         q_re, q_im = probe[0], probe[1]
         p_re = q_re * x_re - q_im * x_im
         p_im = q_re * x_im + q_im * x_re
-        f_re, f_im = from_right(v_hi, v_lo, *from_left(u_hi, u_lo, p_re, p_im))
+        f_re, f_im = from_right(v_below, *from_left(u_beside, p_re, p_im))
         amplitude = 0.05 * jnp.sqrt(counts[s].astype(jnp.float32))
         factor = amplitude * lax.rsqrt(jnp.maximum(f_re * f_re + f_im * f_im, 0.0625))
-        b_re, b_im = from_right(u_hi, u_lo, *from_left(v_hi, v_lo, f_re * factor, f_im * factor))
+        b_re, b_im = from_right(u_below, *from_left(v_beside, f_re * factor, f_im * factor))
         d_re, d_im = b_re - p_re, b_im - p_im
         deposit(0, q_re * d_re + q_im * d_im)
         deposit(1, q_re * d_im - q_im * d_re)
@@ -484,7 +482,8 @@
         scratch_shapes=[
             pltpu.VMEM((3, size, size), f32),
             pltpu.VMEM(((cols + 2 * size) // 128, rows + 2 * size, 128), f32),
-        ] + [pltpu.VMEM((2 * size, 2 * size), jnp.bfloat16)] * 4 + [
+        ] + [pltpu.VMEM((2 * size, 6 * size), jnp.bfloat16)] * 2 + [
+            pltpu.VMEM((6 * size, 2 * size), jnp.bfloat16)] * 2 + [
             pltpu.VMEM((2, (cols + size) // 128, rows + size, 128), f32)] * 2 + [
             dma(((cols + size) // 128, 3)), dma(((cols + size) // 128,))],
         compiler_params=pltpu.CompilerParams(vmem_limit_bytes=VMEM_LIMIT),

time: 74.6 us -> 75.8 us (1.016); the launches traced: 74.2 us -> 74.5 us
  no operation moved by 1% of the time
where the time goes in v2:
time: 75.8 us; the launch traced here: 74.5 us
  Pallas kernels  68.8 us (91%)
  local copies, waits for them, and re-layouts  4.33 us (6%)
  between operations  1.34 us (2%)
    pallas_call x1, Pallas kernels, body(): pl.pallas_call(functools.partial(fold_kernel, shape, half), out_shape=(ja...  33.8 us
    pallas_call x1, Pallas kernels, body(): pl.pallas_call(functools.partial(compute_kernel, shape, rows, cols), out_...  22.3 us
    pallas_call x1, Pallas kernels, body(): pl.pallas_call(functools.partial(halo_kernel, shape, half), out_shape=(ja...  12.6 us
    unnamed x12, local copies, waits for them, and re-layouts  3.56 us

profile of v2, /device:TPU:0, one launch (start us, length us, event | category | flops | bytes accessed | tf_op | source)
XLA Modules:
  0.0 74.5 jit_solution(16828681120296907025)
XLA Ops:
  1.3 0.8 %slice_bitcast_fusion.1 = (s32[4]{0:T(128)S(1)}, s32[4]{0:T(128)S(1)}) fusion(s32[4,2]{0,1:T(2,128)} %bitcast.15), kind=kLoop, calls=%fused_computation.2 | loop fusion | bytes 64 | tf_op jit(solution)/shard_map/squeeze | solution.py:453
  2.0 0.1 pad_add_fusion
  2.1 0.0 copy-start
  2.1 1.6 %copy-done = f32[1,2,256,1024]{3,2,1,0:T(8,128)S(1)} copy-done((f32[1,2,256,1024]{3,2,1,0:T(8,128)S(1)}, f32[1,2,256,1024]{3,2,1,0:T(8,128)}, u32[]{:S(2)}) %copy-start) | copy-done | bytes 2097176
  3.7 0.0 copy-start.1
  3.7 0.0 copy-start.2
  3.7 0.0 copy-start.3
  3.7 0.0 copy-start.4
  3.7 12.6 %shard_map.77 = (f32[2,512,1280]{2,1,0:T(8,128)S(1)}, s32[9,8,128]{2,1,0:T(8,128)S(1)}) custom-call(f32[2,256,1024]{2,1,0:T(8,128)S(1)} %bitcast.10, s32[8,128]{1,0:T(8,128)S(1)} %broadcast_in_dim.4.meta), custom_call_target="tpu_custom_call" | custom-call | flops 10000000000 | bytes 2097152 | tf_op jit(solution)/shard_map/pallas_call | solution.py:455
  16.4 0.0 copy-done.1
  16.4 0.0 copy-done.2
  16.4 0.0 copy-done.3
  16.4 0.0 copy-done.4
  16.4 22.3 %shard_map.78 = (f32[2,512,1280]{2,1,0:T(8,128)S(1)}, f32[256,1024]{1,0:T(8,128)S(1)}, f32[8,128]{1,0:T(8,128)S(1)}, f32[2,4,96,256]{3,2,1,0:T(8,128)S(1)}) custom-call(s32[9,8,128]{2,1,0:T(8,128)S(1)} %get-tuple-element.10.metas, f32[2,256,1024]{2,1,0:T(8,128)S(1)} %bitcast.11, f32[2,512,1280]{2,1,0:T(8,128)S(1)} %get-tuple-element.11.wide_in, ...), custom_call_target="tpu_custom_call" | custom-call | tf_op jit(solution)/shard_map/pallas_call | solution.py:472
  38.8 33.8 %shard_map.79 = (f32[2,256,1024]{2,1,0:T(8,128)S(1)}, f32[2,32,256]{2,1,0:T(8,128)S(1)}) custom-call(f32[2,256,1024]{2,1,0:T(8,128)S(1)} %bitcast.12, f32[2,512,1280]{2,1,0:T(8,128)S(1)} %get-tuple-element.12.tot, f32[256,1024]{1,0:T(8,128)S(1)} %get-tuple-element.13.den_in, f32[8,128]{1,0:T(8,128)S(1)} %get-tuple-element.14.den_max, ...), custom_call_target="tpu_custom_call" | custom-call | tf_op jit(solution)/shard_map/pallas_call | solution.py:492
  72.6 1.3 %copy.11 = f32[1,2,256,1024]{3,2,1,0:T(8,128)} copy(f32[1,2,256,1024]{3,2,1,0:T(8,128)S(1)} %bitcast.13) | data formatting | bytes 4194304
  73.9 0.6 copy.12
  (2 shorter events, 0.0 us)
Async XLA Ops:
  2.1 1.6 %copy-start = (f32[1,2,256,1024]{3,2,1,0:T(8,128)S(1)}, f32[1,2,256,1024]{3,2,1,0:T(8,128)}, u32[]{:S(2)}) copy-start(f32[1,2,256,1024]{3,2,1,0:T(8,128)} %param.6) | copy-start | bytes 6291460
  3.7 12.7 %copy-start.1 = (f32[1,2,256,1024]{3,2,1,0:T(8,128)S(1)}, f32[1,2,256,1024]{3,2,1,0:T(8,128)}, u32[]{:S(2)}) copy-start(f32[1,2,256,1024]{3,2,1,0:T(8,128)} %param.6) | copy-start | bytes 6291460
  3.7 12.7 %copy-start.2 = (f32[2,256,256]{2,1,0:T(8,128)S(1)}, f32[2,256,256]{2,1,0:T(8,128)}, u32[]{:S(2)}) copy-start(f32[2,256,256]{2,1,0:T(8,128)} %probe_in.1) | copy-start | bytes 1572868
  3.7 12.7 %copy-start.3 = (s32[1,1,1,4,256,256]{5,4,3,2,1,0:T(8,128)S(1)}, s32[1,1,1,4,256,256]{5,4,3,2,1,0:T(8,128)}, u32[]{:S(2)}) copy-start(s32[1,1,1,4,256,256]{5,4,3,2,1,0:T(8,128)} %param.10) | copy-start | bytes 3145732
  3.7 12.7 %copy-start.4 = (bf16[4,256,256]{2,1,0:T(8,128)(2,1)S(1)}, bf16[4,256,256]{2,1,0:T(8,128)(2,1)}, u32[]{:S(2)}) copy-start(bf16[4,256,256]{2,1,0:T(8,128)(2,1)} %constant.4.clone.tables) | copy-start | bytes 1572868
